TPU v7x, 32 devices: a whole 2x2x4 slice. The times are simulated.
32 devices in a mesh: dp: 4 (over x, core), expert: 4 (over z), etp: 2 (over y).
Axes of the slice: x: 2, y: 2, z: 4, core: 2. Of those that a mesh axis runs over, the one named last changes fastest.
Arguments:
- tokens: bfloat16 [4096, 3072], P(('dp', 'expert'), 'etp'), parts along dimension 0, may hold values from -6 to 6
- experts: int32 [4096, 2], P(('dp', 'expert')), parts along dimension 0, may hold values from 0 to 3, all different within a row; in each aligned block of 256 rows (0 to 255, 256 to 511, ...) at most 176 rows name the same one
- mixing: float32 [4096, 2], P(('dp', 'expert')), parts along dimension 0, may hold values from 0.2 to 1
- up_weight: bfloat16 [4, 3072, 8192], P('expert', None, 'etp'), may hold values from -0.109375 to 0.109375
- down_weight: bfloat16 [4, 8192, 3072], P('expert', 'etp'), may hold values from -0.0625 to 0.0625
Outputs:
- mixed: bfloat16 [4096, 3072], P(('dp', 'expert'), 'etp'), parts along dimension 0
There are 4 independent parts, one for each index of `dp`. A program takes and returns all parts, laid end to end along the dimension named above; an argument that names none is the same for every part. Nothing has to cross between parts.
Inputs may be any that keep to these rules, and one draw needn't show every extreme that they name: Each row names two different experts. In the rows of one index of expert (aligned blocks of 256 rows) no expert is named more than 176 times, a bound that some block reaches.
All inputs are finite; a program needn't handle non-finite values.
Results may differ from a plain program's by a relative error of at most 0.0078.
Values may be sent and summed in bfloat16 or wider, within the bound.
A program may use at most 128 MiB of HBM per device.

v0:
```python
import functools

import jax
import jax.numpy as jnp
from jax import lax
from jax.experimental import pallas as pl
from jax.experimental.pallas import tpu as pltpu
from jax.sharding import PartitionSpec as P

MESH = pl.DeviceIdType.MESH


def flipped(index, shift, count):
    total, bit = 0, 1
    while bit < count:
        digit = lax.rem(lax.div(index, bit), 2)
        total = total + (1 - digit if shift & bit else digit) * bit
        bit *= 2
    return total


def layer_kernel(
    chunks, sharers, tile,
    tok_ref, routes_ref, up_ref, down_ref, out_ref, share_ref,
    up_v, down_v, full, hidden, other, own, landed, share_v,
    up_sem, down_sem, local_sem,
    zs_sem, zr_sem, ys_sem, yr_sem, bs_sem, br_sem, os_sem, or_sem,
):
    rows, width = tok_ref.shape
    capacity = full.shape[1]
    units = up_v.shape[1]
    my_z = lax.axis_index("expert")
    my_y = lax.axis_index("etp")
    z_index = [flipped(my_z, s, chunks) for s in range(chunks)]
    z_peer = [{"expert": z_index[s]} for s in range(chunks)]
    y_index = [flipped(my_y, t, sharers) for t in range(sharers)]
    y_peer = [{"etp": y_index[t]} for t in range(sharers)]
    cut = -(-capacity // 32) * 16
    pieces = [pl.ds(0, cut), pl.ds(cut, capacity - cut)]
    both = range(len(pieces))

    def remote(src, dst, send, recv, peer):
        return pltpu.make_async_remote_copy(
            src_ref=src, dst_ref=dst, send_sem=send, recv_sem=recv,
            device_id=peer, device_id_type=MESH,
        )

    def columns(t):
        return pl.ds(t * width, width)

    up_copy, down_copy = [], []
    for t in range(sharers):
        begin = pl.multiple_of(y_index[t] * width, 128)
        up_copy.append(
            pltpu.make_async_copy(
                up_ref.at[pl.ds(begin, width), :], up_v.at[columns(t), :], up_sem.at[t]
            )
        )
        down_copy.append(
            pltpu.make_async_copy(
                down_ref.at[:, pl.ds(begin, width)], down_v.at[:, columns(t)], down_sem.at[t]
            )
        )
    for copy in up_copy + down_copy:
        copy.start()

    barrier = pltpu.get_barrier_semaphore()
    for peer in z_peer[1:] + y_peer[1:]:
        pl.semaphore_signal(barrier, inc=1, device_id=peer, device_id_type=MESH)

    z_go = [None] + [
        [
            remote(
                own.at[s, piece], full.at[s, piece, columns(0)],
                zs_sem.at[s, p], zr_sem.at[s, p], z_peer[s],
            )
            for p, piece in enumerate(pieces)
        ]
        for s in range(1, chunks)
    ]
    y_go = [
        [
            [
                remote(
                    full.at[s, piece, columns(0)], full.at[s, piece, columns(t)],
                    ys_sem.at[s, t, p], yr_sem.at[s, t, p], y_peer[t],
                )
                for t in range(1, sharers)
            ]
            for p, piece in enumerate(pieces)
        ]
        for s in range(chunks)
    ]
    y_back = [
        [
            [
                remote(
                    other.at[s, t - 1, piece], landed.at[s, t - 1, piece],
                    bs_sem.at[s, t, p], br_sem.at[s, t, p], y_peer[t],
                )
                for t in range(1, sharers)
            ]
            for p, piece in enumerate(pieces)
        ]
        for s in range(chunks)
    ]
    z_back = [
        pltpu.make_async_copy(own.at[0, piece], out_ref.at[0, piece], local_sem.at[p])
        for p, piece in enumerate(pieces)
    ]
    z_back = [z_back] + [
        [
            remote(
                own.at[s, piece], out_ref.at[s, piece], os_sem.at[s, p], or_sem.at[s, p],
                z_peer[s],
            )
            for p, piece in enumerate(pieces)
        ]
        for s in range(1, chunks)
    ]
    share_copy = pltpu.make_async_copy(share_v, share_ref, local_sem.at[len(pieces)])

    lanes = lax.broadcasted_iota(jnp.int32, (rows, 128), 1).astype(jnp.float32)
    routes = jnp.transpose(routes_ref[...])
    named = [routes[:, k : k + 1] for k in range(2)]
    mixing = [routes[:, k : k + 1] for k in range(2, 4)]
    z_name = [z_index[s].astype(jnp.float32) for s in range(chunks)]
    hot = [jnp.where(lanes == named[k], 1.0, 0.0) for k in range(2)]
    above = jnp.where(
        lax.broadcasted_iota(jnp.int32, (rows, rows), 0)
        > lax.broadcasted_iota(jnp.int32, (rows, rows), 1),
        1.0, 0.0,
    ).astype(jnp.bfloat16)
    counts = [
        jnp.dot(above, hot[k].astype(jnp.bfloat16), preferred_element_type=jnp.float32)
        for k in range(2)
    ]
    counts[1] = counts[1] + jnp.sum(hot[0], axis=0, keepdims=True)
    place = [jnp.sum(counts[k] * hot[k], axis=1, keepdims=True) for k in range(2)]

    def dispatch(s):
        slots = lax.broadcasted_iota(jnp.int32, (rows, capacity), 1).astype(jnp.float32)
        hit = jnp.zeros((rows, capacity), jnp.float32)
        for k in range(2):
            mine = jnp.where(named[k] == z_name[s], place[k], -1.0)
            hit = hit + jnp.where(slots == mine, 1.0, 0.0)
        chunk = lax.dot_general(
            hit.astype(jnp.bfloat16), tok_ref[...], (((0,), (0,)), ((), ())),
            preferred_element_type=jnp.float32,
        ).astype(jnp.bfloat16)
        if s:
            own[s] = chunk
        else:
            full[0, :, columns(0)] = chunk

    def forward(s, p):
        z_go[s][p].wait_recv()
        for copy in y_go[s][p]:
            copy.start()

    def up(s):
        @pl.loop(0, units // tile)
        def _(i):
            at = pl.ds(pl.multiple_of(i * tile, tile), tile)
            value = jnp.dot(full[s], up_v[:, at], preferred_element_type=jnp.float32)
            hidden[:, at] = (value / (1.0 + jnp.exp(-value))).astype(jnp.bfloat16)

    def down(s, t):
        target = other.at[s, t - 1] if t else own.at[s]

        @pl.loop(0, width // tile)
        def _(i):
            at = pl.multiple_of(i * tile, tile)
            value = jnp.dot(
                hidden[...], down_v[:, pl.ds(t * width + at, tile)],
                preferred_element_type=jnp.float32,
            )
            target[:, pl.ds(at, tile)] = value.astype(jnp.bfloat16)

    def start_back(s):
        for p in both:
            for copy in y_back[s][p]:
                copy.start()

    def finish(s, p):
        for copy in y_back[s][p]:
            copy.wait_recv()
        total = own[s, pieces[p]].astype(jnp.float32)
        for t in range(1, sharers):
            total = total + landed[s, t - 1, pieces[p]].astype(jnp.float32)
        own[s, pieces[p]] = total.astype(jnp.bfloat16)
        z_back[s][p].start()

    half = chunks // 2
    order = list(range(chunks))
    dispatch(order[1])
    pl.semaphore_wait(barrier, chunks - 1 + sharers - 1)
    for copy in z_go[order[1]]:
        copy.start()
    for s in [0] + order[2:]:
        dispatch(s)
        for p in both:
            for copy in [z_go[s][p]] if s else y_go[0][p]:
                copy.start()

    slots = lax.broadcasted_iota(jnp.int32, share_v.shape, 1).astype(jnp.float32)
    share = jnp.zeros(share_v.shape, jnp.float32)
    for k in range(2):
        slot = place[k]
        for s in range(1, chunks):
            slot = slot + jnp.where(named[k] == z_name[s], 1.0 * s * capacity, 0.0)
        share = share + jnp.where(slots == slot, mixing[k], 0.0)
    share_v[...] = share.astype(jnp.bfloat16)
    share_copy.start()

    forward(order[1], 0)
    for i, s in enumerate(order):
        for p in both:
            for copy in y_go[s][p]:
                copy.wait_recv()
        if i == 0:
            for copy in up_copy:
                copy.wait()
        up(s)
        if i == 0:
            forward(order[1], 1)
            for copy in down_copy:
                copy.wait()
        elif i + 2 < chunks:
            forward(order[i + 2], 0)
        for t in range(1, sharers):
            down(s, t)
        if s >= half:
            start_back(s)
        if i == chunks - 1:
            for done in order[:-1]:
                if done >= half:
                    for p in both:
                        finish(done, p)
        if s:
            for copy in z_go[s]:
                copy.wait_send()
        down(s, 0)
        if i + 2 < chunks:
            for p in both[1 if i else 0 :]:
                forward(order[i + 2], p)
    rest = list(range(1, half)) + [0]
    for s in rest:
        start_back(s)
    for s in order[-1:] + rest:
        for p in both:
            finish(s, p)

    share_copy.wait()
    for s in range(chunks):
        for p in both:
            for copy in y_go[s][p] + y_back[s][p]:
                copy.wait_send()
            if s:
                z_back[s][p].wait_send()
                z_back[s][p].wait_recv()
            else:
                z_back[s][p].wait()


def run_layer(tokens, routes, up_slab, down_slab, chunks, capacity, sharers):
    rows, width = tokens.shape
    model, units = up_slab.shape
    tile = 512 if width % 512 == 0 else 256
    bf16 = jnp.bfloat16
    dma = pltpu.SemaphoreType.DMA
    anywhere = pl.BlockSpec(memory_space=pl.ANY)
    near = pl.BlockSpec(memory_space=pltpu.VMEM)
    return pl.pallas_call(
        functools.partial(layer_kernel, chunks, sharers, tile),
        out_shape=(
            jax.ShapeDtypeStruct((chunks, capacity, width), bf16),
            jax.ShapeDtypeStruct((rows, chunks * capacity), bf16),
        ),
        in_specs=[near] * 2 + [anywhere] * 2,
        out_specs=(anywhere, anywhere),
        scratch_shapes=[
            pltpu.VMEM((model, units), bf16),
            pltpu.VMEM((units, model), bf16),
            pltpu.VMEM((chunks, capacity, model), bf16),
            pltpu.VMEM((capacity, units), bf16),
            pltpu.VMEM((chunks, sharers - 1, capacity, width), bf16),
            pltpu.VMEM((chunks, capacity, width), bf16),
            pltpu.VMEM((chunks, sharers - 1, capacity, width), bf16),
            pltpu.VMEM((rows, chunks * capacity), bf16),
            dma((sharers,)), dma((sharers,)), dma((3,)),
            dma((chunks, 2)), dma((chunks, 2)),
            dma((chunks, sharers, 2)), dma((chunks, sharers, 2)),
            dma((chunks, sharers, 2)), dma((chunks, sharers, 2)),
            dma((chunks, 2)), dma((chunks, 2)),
        ],
        compiler_params=pltpu.CompilerParams(
            collective_id=0, has_side_effects=True, vmem_limit_bytes=67_043_328
        ),
    )(tokens, routes, up_slab, down_slab)


def local(tokens, experts, mixing, up_weight, down_weight):
    tok_rows, part_width = tokens.shape
    sharers = lax.axis_size("etp")
    expert_count = up_weight.shape[0] * lax.axis_size("expert")
    capacity = 2 * tok_rows // expert_count * 11 // 8
    routes = jnp.concatenate(
        [experts.T.astype(jnp.float32), mixing.T, jnp.zeros((4, tok_rows), jnp.float32)]
    )
    outputs, share = run_layer(
        tokens, routes, up_weight[0], down_weight[0], expert_count, capacity, sharers
    )
    outputs = outputs.reshape(expert_count * capacity, part_width)
    return jnp.dot(share, outputs, preferred_element_type=jnp.float32).astype(jnp.bfloat16)


def solution(mesh):
    placed = (
        P(("dp", "expert"), "etp"),
        P(("dp", "expert"), None),
        P(("dp", "expert"), None),
        P("expert", None, "etp"),
        P("expert", "etp", None),
    )
    return jax.shard_map(
        local, mesh=mesh, in_specs=placed, out_specs=P(("dp", "expert"), "etp"), check_vma=False
    )
```

profile of v0, /device:TPU:0, one launch (start us, length us, event | category | flops | bytes accessed | tf_op | source)
XLA Modules:
  0.0 124.6 jit_solution(2754720694309155319)
XLA Ops:
  0.0 0.1 pad.2.clone
  0.1 0.7 convert_bitcast_fusion
  0.8 1.3 %maximum_maximum_fusion.routes_ref = f32[8,256]{1,0:T(8,128)} fusion(f32[2,256]{1,0:T(2,128)} %bitcast.10, f32[2,256]{1,0:T(2,128)S(1)} %convert_bitcast_fusion, f32[8]{0:T(128)S(1)} %pad.2.clone), kind=kLoop, calls=%fused_computation.1 | loop fusion | flops 4096 | bytes 12320 | tf_op jit(solution)/shard_map/concatenate | solution.py:308
  2.1 119.1 %shard_map.55 = (bf16[4,176,1536]{2,1,0:T(8,128)(2,1)}, bf16[256,704]{1,0:T(8,128)(2,1)}) custom-call(bf16[256,1536]{1,0:T(8,128)(2,1)} %tok_ref.1, f32[8,256]{1,0:T(8,128)} %maximum_maximum_fusion.routes_ref, bf16[3072,4096]{1,0:T(8,128)(2,1)} %bitcast.8, bf16[4096,3072]{1,0:T(8,128)(2,1)} %bitcast.9), custom_call_target="tpu_custom_call" | custom-call | tf_op jit(solution)/shard_map/pallas_call | solution.py:274
  121.2 3.4 %convolution_convert_fusion = bf16[256,1536]{1,0:T(8,128)(2,1)} fusion(bf16[256,704]{1,0:T(8,128)(2,1)} %get-tuple-element.7, bf16[704,1536]{1,0:T(8,128)(2,1)} %bitcast.11), kind=kOutput, calls=%fused_computation | convolution fusion | flops 554041344 | bytes 3309568 | tf_op jit(solution)/shard_map/dot_general | solution.py:315
  (1 shorter events, 0.0 us)
where the time goes:
time: 125 us
  Pallas kernels  119 us (95%)
  matrix products  3.41 us (3%)
  other arithmetic  2.03 us (2%)
    pallas_call x1, Pallas kernels, run_layer(): pl.pallas_call(functools.partial(layer_kernel, chunks, sharers, tile), ou...  119 us
    dot_general x1, matrix products, local(): jnp.dot(share, outputs, preferred_element_type=jnp.float32)  3.41 us

commit v1 on v0

v1 whole, which is shorter than its diff:
```python
import functools

import jax
import jax.numpy as jnp
from jax import lax
from jax.experimental import pallas as pl
from jax.experimental.pallas import tpu as pltpu
from jax.sharding import PartitionSpec as P

MESH = pl.DeviceIdType.MESH
HALVES = 2

TUNED = {
    4: (
        "D0-D1-D3-F00F10",
        "U00V00W00F11F30",
        "U10D2-V10F31W10Y10",
        "U11V11W11F20",
        "U30V30W30Z10Y30",
        "U31V31Y31Z30W31F21F01",
        "U20Y11V20Z31W20Y20",
        "U21V21Y00Z20W21Y21Z11",
        "U01V01W01Z21Y01Z01Z00",
    ),
}


def plan(chunks):
    if chunks in TUNED:
        text = "".join(TUNED[chunks])
        return [
            (text[i], int(text[i + 1]), 0 if text[i + 2] == "-" else int(text[i + 2]))
            for i in range(0, len(text), 3)
        ]
    halves, order = range(HALVES), range(chunks)
    actions = [("D", s, 0) for s in order]
    actions += [("F", s, h) for s in order[:2] for h in halves]
    for s in order:
        actions += [(kind, s, h) for h in halves for kind in "UVYW"]
        actions += [("F", s + 2, h) for h in halves if s + 2 < chunks]
    return actions + [("Z", s, h) for s in reversed(order) for h in halves]


def flipped(index, shift, count):
    total, bit = 0, 1
    while bit < count:
        digit = lax.rem(lax.div(index, bit), 2)
        total = total + (1 - digit if shift & bit else digit) * bit
        bit *= 2
    return total


def layer_kernel(
    chunks, sharers, capacity, actions,
    tok_ref, experts_ref, mixing_ref, up_ref, down_ref, out_ref, share_ref,
    up_v, down_v, full, hidden, other, own, landed, share_v,
    up_sem, down_sem, local_sem,
    zs_sem, zr_sem, ys_sem, yr_sem, bs_sem, br_sem, os_sem, or_sem,
):
    rows, width = tok_ref.shape
    cut, units = hidden.shape
    my_z = lax.axis_index("expert")
    my_y = lax.axis_index("etp")
    z_index = [flipped(my_z, s, chunks) for s in range(chunks)]
    z_peer = [{"expert": z_index[s]} for s in range(chunks)]
    y_index = [flipped(my_y, t, sharers) for t in range(sharers)]
    y_peer = [{"etp": y_index[t]} for t in range(sharers)]
    pieces = [pl.ds(0, cut), pl.ds(cut, capacity - cut)]
    both = range(HALVES)

    def remote(src, dst, send, recv, peer):
        return pltpu.make_async_remote_copy(
            src_ref=src, dst_ref=dst, send_sem=send, recv_sem=recv,
            device_id=peer, device_id_type=MESH,
        )

    def columns(t):
        return pl.ds(t * width, width)

    up_copy, down_copy = [], []
    for t in range(sharers):
        begin = pl.multiple_of(y_index[t] * width, 128)
        up_copy.append(
            pltpu.make_async_copy(
                up_ref.at[pl.ds(begin, width), :], up_v.at[columns(t), :], up_sem.at[t]
            )
        )
        down_copy.append(
            pltpu.make_async_copy(
                down_ref.at[:, pl.ds(begin, width)], down_v.at[:, columns(t)], down_sem.at[t]
            )
        )
    for copy in up_copy + down_copy:
        copy.start()

    barrier = pltpu.get_barrier_semaphore()
    for peer in z_peer[1:] + y_peer[1:]:
        pl.semaphore_signal(barrier, inc=1, device_id=peer, device_id_type=MESH)

    def z_go(s, p):
        return remote(
            own.at[s, pieces[p]], full.at[s, pieces[p], columns(0)],
            zs_sem.at[s, p], zr_sem.at[s, p], z_peer[s],
        )

    def y_go(s, p):
        return [
            remote(
                full.at[s, pieces[p], columns(0)], full.at[s, pieces[p], columns(t)],
                ys_sem.at[s, t, p], yr_sem.at[s, t, p], y_peer[t],
            )
            for t in range(1, sharers)
        ]

    def y_back(s, p):
        return [
            remote(
                other.at[s, t - 1, pieces[p]], landed.at[s, t - 1, pieces[p]],
                bs_sem.at[s, t, p], br_sem.at[s, t, p], y_peer[t],
            )
            for t in range(1, sharers)
        ]

    def z_back(s, p):
        if s == 0:
            return pltpu.make_async_copy(
                own.at[0, pieces[p]], out_ref.at[0, pieces[p]], local_sem.at[p]
            )
        return remote(
            own.at[s, pieces[p]], out_ref.at[s, pieces[p]], os_sem.at[s, p], or_sem.at[s, p],
            z_peer[s],
        )

    share_copy = pltpu.make_async_copy(share_v, share_ref, local_sem.at[HALVES])

    names = experts_ref[...].astype(jnp.float32)
    named = [names[k : k + 1] for k in range(2)]
    mixing = [mixing_ref[k : k + 1, :] for k in range(2)]
    z_name = [z_index[s].astype(jnp.float32) for s in range(chunks)]
    kinds = -(-chunks // 16) * 16
    label = lax.broadcasted_iota(jnp.int32, (kinds, rows), 0).astype(jnp.float32)
    hot = [jnp.where(label == named[k], 1.0, 0.0) for k in range(2)]
    ahead = jnp.where(
        lax.broadcasted_iota(jnp.int32, (rows, rows), 0)
        < lax.broadcasted_iota(jnp.int32, (rows, rows), 1),
        1.0, 0.0,
    ).astype(jnp.bfloat16)
    counts = [
        jnp.dot(hot[k].astype(jnp.bfloat16), ahead, preferred_element_type=jnp.float32)
        for k in range(2)
    ]
    counts[1] = counts[1] + jnp.sum(hot[0], axis=1, keepdims=True)
    place = [jnp.sum(counts[k] * hot[k], axis=0, keepdims=True) for k in range(2)]
    slots = lax.broadcasted_iota(jnp.int32, (capacity, rows), 0).astype(jnp.float32)

    def taken(s, values):
        hit = jnp.zeros((capacity, rows), jnp.float32)
        for k in range(2):
            mine = jnp.where(named[k] == z_name[s], place[k], -1.0)
            hit = hit + jnp.where(slots == mine, values[k], 0.0)
        return hit.astype(jnp.bfloat16)

    greeted = []

    def dispatch(s):
        chunk = jnp.dot(
            taken(s, [1.0, 1.0]), tok_ref[...], preferred_element_type=jnp.float32
        ).astype(jnp.bfloat16)
        if s:
            own[s, pl.ds(0, capacity)] = chunk
        else:
            full[0, pl.ds(0, capacity), columns(0)] = chunk
        if not greeted:
            pl.semaphore_wait(barrier, chunks - 1 + sharers - 1)
            greeted.append(s)
        for p in both:
            for copy in [z_go(s, p)] if s else y_go(0, p):
                copy.start()

    def forward(s, p):
        if s:
            z_go(s, p).wait_recv()
            for copy in y_go(s, p):
                copy.start()

    def finish(s, p):
        for copy in y_back(s, p):
            copy.wait_recv()
        total = own[s, pieces[p]].astype(jnp.float32)
        for t in range(1, sharers):
            total = total + landed[s, t - 1, pieces[p]].astype(jnp.float32)
        own[s, pieces[p]] = total.astype(jnp.bfloat16)
        z_back(s, p).start()

    def send_other(s, p):
        for copy in y_back(s, p):
            copy.start()

    act = {"D": lambda s, p: dispatch(s), "F": forward, "Y": send_other, "Z": finish}

    steps, slot = [], None
    lead = []
    for kind, s, p in actions:
        if kind == "U":
            steps.append(((s, p), [[], [], []]))
            slot = 0
        elif kind in "VW":
            slot = "UVW".index(kind)
        elif not steps:
            lead.append((kind, s, p))
        else:
            steps[-1][1][slot].append((kind, s, p))

    def pick(n, values):
        total = 0
        for k, value in enumerate(values):
            if value:
                total = total + jnp.where(n == k, value, 0)
        return jnp.int32(total)

    for kind, s, p in lead:
        act[kind](s, p)
    share_v[...] = jnp.concatenate([taken(s, mixing) for s in range(chunks)])
    share_copy.start()

    @pl.loop(0, len(steps))
    def _(n):
        chunk = pick(n, [unit[0] for unit, _ in steps])
        at_row = pl.ds(pl.multiple_of(pick(n, [unit[1] * cut for unit, _ in steps]), cut), cut)

        def during(slot):
            for k, (_, slots) in enumerate(steps):
                if slots[slot]:
                    @pl.when(n == k)
                    def _():
                        for kind, s, p in slots[slot]:
                            act[kind](s, p)

        for k, (unit, _) in enumerate(steps):
            @pl.when(n == k)
            def _():
                for copy in y_go(*unit):
                    copy.wait_recv()
                if k == 0:
                    for copy in up_copy:
                        copy.wait()

        tile = 2048 if units % 2048 == 0 else 256

        @pl.loop(0, units // tile)
        def _(i):
            at = pl.ds(pl.multiple_of(i * tile, tile), tile)
            value = jnp.dot(full[chunk, at_row], up_v[:, at], preferred_element_type=jnp.float32)
            hidden[:, at] = (value / (1.0 + jnp.exp(-value))).astype(jnp.bfloat16)

        during(0)

        @pl.when(n == 0)
        def _():
            for copy in down_copy:
                copy.wait()

        for t in range(1, sharers):
            other[chunk, t - 1, at_row] = jnp.dot(
                hidden[...], down_v[:, columns(t)], preferred_element_type=jnp.float32
            ).astype(jnp.bfloat16)
        during(1)
        for k, ((s, p), _) in enumerate(steps):
            if s:
                @pl.when(n == k)
                def _():
                    z_go(s, p).wait_send()
        own[chunk, at_row] = jnp.dot(
            hidden[...], down_v[:, columns(0)], preferred_element_type=jnp.float32
        ).astype(jnp.bfloat16)
        during(2)

    share_copy.wait()
    for s in range(chunks):
        for p in both:
            for copy in y_go(s, p) + y_back(s, p):
                copy.wait_send()
            if s:
                z_back(s, p).wait_send()
                z_back(s, p).wait_recv()
            else:
                z_back(s, p).wait()


def run_layer(tokens, experts, mixing, up_slab, down_slab, chunks, capacity, sharers):
    rows, width = tokens.shape
    model, units = up_slab.shape
    cut = -(-capacity // (16 * HALVES)) * 16
    bf16 = jnp.bfloat16
    dma = pltpu.SemaphoreType.DMA
    anywhere = pl.BlockSpec(memory_space=pl.ANY)
    near = pl.BlockSpec(memory_space=pltpu.VMEM)
    return pl.pallas_call(
        functools.partial(layer_kernel, chunks, sharers, capacity, plan(chunks)),
        out_shape=(
            jax.ShapeDtypeStruct((chunks, capacity, width), bf16),
            jax.ShapeDtypeStruct((chunks * capacity, rows), bf16),
        ),
        in_specs=[near] * 3 + [anywhere] * 2,
        out_specs=(anywhere, anywhere),
        scratch_shapes=[
            pltpu.VMEM((model, units), bf16),
            pltpu.VMEM((units, model), bf16),
            pltpu.VMEM((chunks, HALVES * cut, model), bf16),
            pltpu.VMEM((cut, units), bf16),
            pltpu.VMEM((chunks, sharers - 1, HALVES * cut, width), bf16),
            pltpu.VMEM((chunks, HALVES * cut, width), bf16),
            pltpu.VMEM((chunks, sharers - 1, capacity, width), bf16),
            pltpu.VMEM((chunks * capacity, rows), bf16),
            dma((sharers,)), dma((sharers,)), dma((3,)),
            dma((chunks, 2)), dma((chunks, 2)),
            dma((chunks, sharers, 2)), dma((chunks, sharers, 2)),
            dma((chunks, sharers, 2)), dma((chunks, sharers, 2)),
            dma((chunks, 2)), dma((chunks, 2)),
        ],
        compiler_params=pltpu.CompilerParams(
            collective_id=0, has_side_effects=True, vmem_limit_bytes=67_043_328
        ),
    )(tokens, experts, mixing, up_slab, down_slab)


def local(tokens, experts, mixing, up_weight, down_weight):
    tok_rows, part_width = tokens.shape
    sharers = lax.axis_size("etp")
    expert_count = up_weight.shape[0] * lax.axis_size("expert")
    capacity = 2 * tok_rows // expert_count * 11 // 8
    outputs, share = run_layer(
        tokens, experts.T, mixing.T, up_weight[0], down_weight[0],
        expert_count, capacity, sharers,
    )
    outputs = outputs.reshape(expert_count * capacity, part_width)
    return lax.dot_general(
        share, outputs, (((0,), (0,)), ((), ())), preferred_element_type=jnp.float32
    ).astype(jnp.bfloat16)


def solution(mesh):
    placed = (
        P(("dp", "expert"), "etp"),
        P(("dp", "expert"), None),
        P(("dp", "expert"), None),
        P("expert", None, "etp"),
        P("expert", "etp", None),
    )
    return jax.shard_map(
        local, mesh=mesh, in_specs=placed, out_specs=P(("dp", "expert"), "etp"), check_vma=False
    )
```

time: 125 us -> 115 us (0.920)
  Pallas kernels: 119 us -> 111 us
  other arithmetic: 2.03 us -> 0 us
    pallas_call x1, Pallas kernels: 119 us -> 111 us  [run_layer(): pl.pallas_call(functools.partial(layer_kernel, chunks, sharers, capacity,...]
    concatenate x1 -> x0, other arithmetic: 1.35 us -> none  [local(): jnp.concatenate([experts.T.astype(jnp.float32), mixing.T, jnp.zeros((4, t...]
where the time goes in v1:
time: 115 us
  Pallas kernels  111 us (97%)
  matrix products  3.42 us (3%)
    pallas_call x1, Pallas kernels, run_layer(): pl.pallas_call(functools.partial(layer_kernel, chunks, sharers, capacity,...  111 us
    dot_general x1, matrix products, local(): lax.dot_general(share, outputs, (((0,), (0,)), ((), ())), preferred_eleme...  3.42 us

profile of v1, /device:TPU:0, one launch (start us, length us, event | category | flops | bytes accessed | tf_op | source)
XLA Modules:
  0.0 114.7 jit_solution(8439423088339065244)
XLA Ops:
  0.0 111.3 %shard_map.55 = (bf16[4,176,1536]{2,1,0:T(8,128)(2,1)}, bf16[704,256]{1,0:T(8,128)(2,1)}) custom-call(bf16[256,1536]{1,0:T(8,128)(2,1)} %tok_ref.1, s32[2,256]{1,0:T(2,128)} %bitcast.10, f32[2,256]{1,0:T(2,128)} %bitcast.11, bf16[3072,4096]{1,0:T(8,128)(2,1)} %bitcast.7, bf16[4096,3072]{1,0:T(8,128)(2,1)} %bitcast.8), custom_call_target="tpu_custom_call" | custom-call | tf_op jit(solution)/shard_map/pallas_call | solution.py:298
  111.3 3.4 %convolution_convert_fusion = bf16[256,1536]{1,0:T(8,128)(2,1)} fusion(bf16[704,256]{1,0:T(8,128)(2,1)} %get-tuple-element.7, bf16[704,1536]{1,0:T(8,128)(2,1)} %bitcast.9), kind=kOutput, calls=%fused_computation | convolution fusion | flops 554041344 | bytes 3309568 | tf_op jit(solution)/shard_map/dot_general | solution.py:337

commit v2 on v1

--- a/solution.py
+++ b/solution.py
@@ -12,15 +12,15 @@
 
 TUNED = {
     4: (
-        "D0-D1-D3-F00F10",
-        "U00V00W00F11F30",
-        "U10D2-V10F31W10Y10",
-        "U11V11W11F20",
-        "U30V30W30Z10Y30",
-        "U31V31Y31Z30W31F21F01",
-        "U20Y11V20Z31W20Y20",
-        "U21V21Y00Z20W21Y21Z11",
-        "U01V01W01Z21Y01Z01Z00",
+        "D0-D1-D3-F10",
+        "U00V00W00D2-F30",
+        "U10V10F11Y10W10",
+        "U30V30F31Y30W30",
+        "U11V11Z10W11F20",
+        "U31Z30V31Y31W31F21",
+        "U20Z31V20Y20W20",
+        "U21Y11Z20V21Y21W21Z11Y00",
+        "U01V01Z21W01Y01Z01Z00",
     ),
 }
 
@@ -58,7 +58,8 @@
     zs_sem, zr_sem, ys_sem, yr_sem, bs_sem, br_sem, os_sem, or_sem,
 ):
     rows, width = tok_ref.shape
-    cut, units = hidden.shape
+    units = hidden.shape[1]
+    cut = full.shape[1] // HALVES
     my_z = lax.axis_index("expert")
     my_y = lax.axis_index("etp")
     z_index = [flipped(my_z, s, chunks) for s in range(chunks)]
@@ -223,10 +224,14 @@
     share_v[...] = jnp.concatenate([taken(s, mixing) for s in range(chunks)])
     share_copy.start()
 
+    tile = 2048 if units % 2048 == 0 else 256
+    shapes = [(unit[1] == HALVES, unit) for unit, _ in steps]
+
     @pl.loop(0, len(steps))
     def _(n):
-        chunk = pick(n, [unit[0] for unit, _ in steps])
-        at_row = pl.ds(pl.multiple_of(pick(n, [unit[1] * cut for unit, _ in steps]), cut), cut)
+        chunk = pick(n, [unit[0] for _, unit in shapes])
+        begin = pick(n, [unit[1] * cut if not big else 0 for big, unit in shapes])
+        whole = pick(n, [int(big) for big, _ in shapes]) == 1
 
         def during(slot):
             for k, (_, slots) in enumerate(steps):
@@ -236,22 +241,35 @@
                         for kind, s, p in slots[slot]:
                             act[kind](s, p)
 
-        for k, (unit, _) in enumerate(steps):
+        def sized(compute):
+            if any(big for big, _ in shapes):
+                @pl.when(whole)
+                def _():
+                    compute(pl.ds(0, capacity), pl.ds(0, capacity))
+            if not all(big for big, _ in shapes):
+                @pl.when(jnp.logical_not(whole))
+                def _():
+                    compute(pl.ds(pl.multiple_of(begin, cut), cut), pl.ds(0, cut))
+
+        for k, (big, (s, h)) in enumerate(shapes):
             @pl.when(n == k)
             def _():
-                for copy in y_go(*unit):
-                    copy.wait_recv()
+                for p in both if big else [h]:
+                    for copy in y_go(s, p):
+                        copy.wait_recv()
                 if k == 0:
                     for copy in up_copy:
                         copy.wait()
 
-        tile = 2048 if units % 2048 == 0 else 256
-
-        @pl.loop(0, units // tile)
-        def _(i):
-            at = pl.ds(pl.multiple_of(i * tile, tile), tile)
-            value = jnp.dot(full[chunk, at_row], up_v[:, at], preferred_element_type=jnp.float32)
-            hidden[:, at] = (value / (1.0 + jnp.exp(-value))).astype(jnp.bfloat16)
+        @sized
+        def _(at_row, top):
+            @pl.loop(0, units // tile)
+            def _(i):
+                at = pl.ds(pl.multiple_of(i * tile, tile), tile)
+                value = jnp.dot(
+                    full[chunk, at_row], up_v[:, at], preferred_element_type=jnp.float32
+                )
+                hidden[top, at] = (value / (1.0 + jnp.exp(-value))).astype(jnp.bfloat16)
 
         during(0)
 
@@ -260,19 +278,27 @@
             for copy in down_copy:
                 copy.wait()
 
-        for t in range(1, sharers):
-            other[chunk, t - 1, at_row] = jnp.dot(
-                hidden[...], down_v[:, columns(t)], preferred_element_type=jnp.float32
-            ).astype(jnp.bfloat16)
+        @sized
+        def _(at_row, top):
+            for t in range(1, sharers):
+                other[chunk, t - 1, at_row] = jnp.dot(
+                    hidden[top], down_v[:, columns(t)], preferred_element_type=jnp.float32
+                ).astype(jnp.bfloat16)
+
         during(1)
-        for k, ((s, p), _) in enumerate(steps):
+        for k, (big, (s, h)) in enumerate(shapes):
             if s:
                 @pl.when(n == k)
                 def _():
-                    z_go(s, p).wait_send()
-        own[chunk, at_row] = jnp.dot(
-            hidden[...], down_v[:, columns(0)], preferred_element_type=jnp.float32
-        ).astype(jnp.bfloat16)
+                    for p in both if big else [h]:
+                        z_go(s, p).wait_send()
+
+        @sized
+        def _(at_row, top):
+            own[chunk, at_row] = jnp.dot(
+                hidden[top], down_v[:, columns(0)], preferred_element_type=jnp.float32
+            ).astype(jnp.bfloat16)
+
         during(2)
 
     share_copy.wait()
@@ -291,12 +317,15 @@
     rows, width = tokens.shape
     model, units = up_slab.shape
     cut = -(-capacity // (16 * HALVES)) * 16
+    actions = plan(chunks)
+    whole = any(kind == "U" and h == HALVES for kind, _, h in actions)
+    most = capacity if whole else cut
     bf16 = jnp.bfloat16
     dma = pltpu.SemaphoreType.DMA
     anywhere = pl.BlockSpec(memory_space=pl.ANY)
     near = pl.BlockSpec(memory_space=pltpu.VMEM)
     return pl.pallas_call(
-        functools.partial(layer_kernel, chunks, sharers, capacity, plan(chunks)),
+        functools.partial(layer_kernel, chunks, sharers, capacity, actions),
         out_shape=(
             jax.ShapeDtypeStruct((chunks, capacity, width), bf16),
             jax.ShapeDtypeStruct((chunks * capacity, rows), bf16),
@@ -307,7 +336,7 @@
             pltpu.VMEM((model, units), bf16),
             pltpu.VMEM((units, model), bf16),
             pltpu.VMEM((chunks, HALVES * cut, model), bf16),
-            pltpu.VMEM((cut, units), bf16),
+            pltpu.VMEM((max(most, cut), units), bf16),
             pltpu.VMEM((chunks, sharers - 1, HALVES * cut, width), bf16),
             pltpu.VMEM((chunks, HALVES * cut, width), bf16),
             pltpu.VMEM((chunks, sharers - 1, capacity, width), bf16),

time: 115 us -> 109 us (0.948)
  Pallas kernels: 111 us -> 106 us
    pallas_call x1, Pallas kernels: 111 us -> 106 us  [run_layer(): pl.pallas_call(functools.partial(layer_kernel, chunks, sharers, capacity,...]
where the time goes in v2:
time: 109 us
  Pallas kernels  106 us (97%)
  matrix products  3.42 us (3%)
    pallas_call x1, Pallas kernels, run_layer(): pl.pallas_call(functools.partial(layer_kernel, chunks, sharers, capacity,...  106 us
    dot_general x1, matrix products, local(): lax.dot_general(share, outputs, (((0,), (0,)), ((), ())), preferred_eleme...  3.42 us

profile of v2, /device:TPU:0, one launch (start us, length us, event | category | flops | bytes accessed | tf_op | source)
XLA Modules:
  0.0 109.1 jit_solution(16707713657800680475)
XLA Ops:
  0.0 105.7 %shard_map.55 = (bf16[4,176,1536]{2,1,0:T(8,128)(2,1)}, bf16[704,256]{1,0:T(8,128)(2,1)}) custom-call(bf16[256,1536]{1,0:T(8,128)(2,1)} %tok_ref.1, s32[2,256]{1,0:T(2,128)} %bitcast.10, f32[2,256]{1,0:T(2,128)} %bitcast.11, bf16[3072,4096]{1,0:T(8,128)(2,1)} %bitcast.7, bf16[4096,3072]{1,0:T(8,128)(2,1)} %bitcast.8), custom_call_target="tpu_custom_call" | custom-call | tf_op jit(solution)/shard_map/pallas_call | solution.py:327
  105.7 3.4 %convolution_convert_fusion = bf16[256,1536]{1,0:T(8,128)(2,1)} fusion(bf16[704,256]{1,0:T(8,128)(2,1)} %get-tuple-element.7, bf16[704,1536]{1,0:T(8,128)(2,1)} %bitcast.9), kind=kOutput, calls=%fused_computation | convolution fusion | flops 554041344 | bytes 3309568 | tf_op jit(solution)/shard_map/dot_general | solution.py:366

commit v3 on v1

--- a/solution.py
+++ b/solution.py
@@ -12,15 +12,15 @@
 
 TUNED = {
     4: (
-        "D0-D1-D3-F00F10",
-        "U00V00W00F11F30",
-        "U10D2-V10F31W10Y10",
-        "U11V11W11F20",
-        "U30V30W30Z10Y30",
-        "U31V31Y31Z30W31F21F01",
-        "U20Y11V20Z31W20Y20",
-        "U21V21Y00Z20W21Y21Z11",
-        "U01V01W01Z21Y01Z01Z00",
+        "D0-D1-D3-F10",
+        "U00V00F30W00F11",
+        "U10V10D2-F31W10",
+        "U30V30Y30W30Y10",
+        "U31V31F20Z30W31",
+        "U11Z10Y31V11W11F21",
+        "U20Z31V20Y20Y11W20",
+        "U21V21Z20Y21Y00W21Z11",
+        "U01V01Y01Z21Z00W01Z01",
     ),
 }
 

time: 115 us -> 108 us (0.939)
  Pallas kernels: 111 us -> 104 us
    pallas_call x1, Pallas kernels: 111 us -> 104 us  [run_layer(): pl.pallas_call(functools.partial(layer_kernel, chunks, sharers, capacity,...]
where the time goes in v3:
time: 108 us
  Pallas kernels  104 us (96%)
  matrix products  3.42 us (3%)
    pallas_call x1, Pallas kernels, run_layer(): pl.pallas_call(functools.partial(layer_kernel, chunks, sharers, capacity,...  104 us
    dot_general x1, matrix products, local(): lax.dot_general(share, outputs, (((0,), (0,)), ((), ())), preferred_eleme...  3.42 us

profile of v3, /device:TPU:0, one launch (start us, length us, event | category | flops | bytes accessed | tf_op | source)
XLA Modules:
  0.0 107.9 jit_solution(1090224518402303887)
XLA Ops:
  0.0 104.5 %shard_map.55 = (bf16[4,176,1536]{2,1,0:T(8,128)(2,1)}, bf16[704,256]{1,0:T(8,128)(2,1)}) custom-call(bf16[256,1536]{1,0:T(8,128)(2,1)} %tok_ref.1, s32[2,256]{1,0:T(2,128)} %bitcast.10, f32[2,256]{1,0:T(2,128)} %bitcast.11, bf16[3072,4096]{1,0:T(8,128)(2,1)} %bitcast.7, bf16[4096,3072]{1,0:T(8,128)(2,1)} %bitcast.8), custom_call_target="tpu_custom_call" | custom-call | tf_op jit(solution)/shard_map/pallas_call | solution.py:298
  104.5 3.4 %convolution_convert_fusion = bf16[256,1536]{1,0:T(8,128)(2,1)} fusion(bf16[704,256]{1,0:T(8,128)(2,1)} %get-tuple-element.7, bf16[704,1536]{1,0:T(8,128)(2,1)} %bitcast.9), kind=kOutput, calls=%fused_computation | convolution fusion | flops 554041344 | bytes 3309568 | tf_op jit(solution)/shard_map/dot_general | solution.py:337

commit v4 on v3

--- a/solution.py
+++ b/solution.py
@@ -18,7 +18,7 @@
         "U30V30Y30W30Y10",
         "U31V31F20Z30W31",
         "U11Z10Y31V11W11F21",
-        "U20Z31V20Y20Y11W20",
+        "U20V20Z31Y20Y11W20",
         "U21V21Z20Y21Y00W21Z11",
         "U01V01Y01Z21Z00W01Z01",
     ),

time: 108 us -> 108 us (level)
  no operation moved by 1% of the time
where the time goes in v4:
time: 108 us
  Pallas kernels  104 us (96%)
  matrix products  3.42 us (3%)
    pallas_call x1, Pallas kernels, run_layer(): pl.pallas_call(functools.partial(layer_kernel, chunks, sharers, capacity,...  104 us
    dot_general x1, matrix products, local(): lax.dot_general(share, outputs, (((0,), (0,)), ((), ())), preferred_eleme...  3.42 us

profile of v4, /device:TPU:0, one launch (start us, length us, event | category | flops | bytes accessed | tf_op | source)
XLA Modules:
  0.0 107.9 jit_solution(12403879690610872176)
XLA Ops:
  0.0 104.5 %shard_map.55 = (bf16[4,176,1536]{2,1,0:T(8,128)(2,1)}, bf16[704,256]{1,0:T(8,128)(2,1)}) custom-call(bf16[256,1536]{1,0:T(8,128)(2,1)} %tok_ref.1, s32[2,256]{1,0:T(2,128)} %bitcast.10, f32[2,256]{1,0:T(2,128)} %bitcast.11, bf16[3072,4096]{1,0:T(8,128)(2,1)} %bitcast.7, bf16[4096,3072]{1,0:T(8,128)(2,1)} %bitcast.8), custom_call_target="tpu_custom_call" | custom-call | tf_op jit(solution)/shard_map/pallas_call | solution.py:298
  104.5 3.4 %convolution_convert_fusion = bf16[256,1536]{1,0:T(8,128)(2,1)} fusion(bf16[704,256]{1,0:T(8,128)(2,1)} %get-tuple-element.7, bf16[704,1536]{1,0:T(8,128)(2,1)} %bitcast.9), kind=kOutput, calls=%fused_computation | convolution fusion | flops 554041344 | bytes 3309568 | tf_op jit(solution)/shard_map/dot_general | solution.py:337
